TPU v7x, 32 devices: a whole 2x2x4 slice. The times are simulated.
32 devices in a mesh: dom: 8 (over z, core), grp: 4 (over y, x).
Axes of the slice: x: 2, y: 2, z: 4, core: 2. Of those that a mesh axis runs over, the one named last changes fastest.
Arguments:
- fine_level_residual: float32 [3, 15, 4096], P(None, None, ('dom', 'grp')), may hold values from -6 to 6
- restriction_matrix: float32 [3, 15], replicated, may hold values from -1.5 to 1.5
- prolongation_matrix: float32 [15, 3], replicated, may hold values from -3.5 to 3.5
- block_inverse: bfloat16 [9, 9, 4096], P(None, None, 'dom')
- face_coupling: bfloat16 [3, 9, 9, 4096], P(None, None, None, 'dom'), may hold values from -1.75 to 1.75
- neighbours: int32 [3, 4096], P(None, 'dom'), may hold values from -512 to 512, as said below
Outputs:
- correction: float32 [3, 15, 4096], P(None, None, ('dom', 'grp'))
Inputs may be any that keep to these rules, and one draw needn't show every extreme that they name: `neighbours`: each entry is 0 or a nonzero offset d with |d| at most 512 such that e + d is another triangle of the grid.
All inputs are finite; a program needn't handle non-finite values.
Results may differ from a plain program's by a relative error of at most 0.0003.
Values sent between devices are 32-bit elements; how exact they have to be, the bound alone decides.
No kernel may reach another device: no remote copies, remote signals or barrier semaphores. Data moves between devices by JAX's collectives and lax.ppermute only.
A program may use at most 64 MiB of HBM per device.

v0:
```python
import functools

import jax
import jax.numpy as jnp
from jax import lax
from jax.experimental import pallas as pl
from jax.experimental.pallas import tpu as pltpu
from jax.sharding import PartitionSpec as P


SWEEPS = 6
damping = 0.8
LANES = 128
SUBLANES = 8
COMP = 9
FACES = 3


class Shape:
    def __init__(self, width):
        self.W = width // LANES
        assert self.W * LANES == width and (self.W == 4 or self.W % 8 == 0)
        self.rows = -(-COMP * self.W // SUBLANES) * SUBLANES
        self.NV = self.rows // SUBLANES
        self.Q = max(1, self.W // SUBLANES)
        self.H = max(1, SUBLANES // self.W)
        self.index_rows = max(SUBLANES, self.W)
        self.table_rows = 2 * COMP * self.W + 2 * SUBLANES if self.H == 1 else 2 * (self.rows + SUBLANES)


def place_of_row(s):
    row = lax.broadcasted_iota(jnp.int32, (SUBLANES, LANES), 0)
    return row & (s.W - 1) if s.H > 1 else row


def load(sources, targets, sems):
    copies = [
        pltpu.make_async_copy(source, target, sems.at[n]) for n, (source, target) in enumerate(zip(sources, targets))
    ]
    for copy in copies:
        copy.start()
    for copy in copies:
        copy.wait()


def restrict_kernel(grp, residual_hbm, restriction_hbm, inverse_hbm, out_ref, residual_ref, restriction_ref, inverse_ref, rhs_ref, sems):
    columns = pl.ds(pl.multiple_of(lax.axis_index(grp) * LANES, LANES), LANES)
    load(
        (residual_hbm, restriction_hbm, inverse_hbm.at[:, :, columns]),
        (residual_ref, restriction_ref, inverse_ref),
        sems,
    )
    nodes = residual_ref.shape[1]
    diagonal = lax.broadcasted_iota(jnp.int32, (nodes, nodes), 0) == lax.broadcasted_iota(
        jnp.int32, (nodes, nodes), 1
    )
    for m in range(3):
        row = jnp.broadcast_to(restriction_ref[m : m + 1, :], (nodes, nodes))
        column = jnp.sum(jnp.where(diagonal, row, 0.0), axis=1, keepdims=True)
        for v in range(3):
            rhs_ref[3 * v + m : 3 * v + m + 1, :] = jnp.sum(
                column * residual_ref[v], axis=0, keepdims=True
            )
    rhs = rhs_ref[...]
    for i in range(COMP):
        out_ref[i : i + 1, :] = damping * jnp.sum(
            inverse_ref[i].astype(jnp.float32) * rhs, axis=0, keepdims=True
        )


def prepare_kernel(s, dom, *refs):
    sources, targets, sems = refs[:3], refs[-4:-1], refs[-1]
    spread_out, coup_out, lane_out, own_out, halo_out, even_out = refs[3:-4]
    inverse_ref, coupling_ref, neighbours_ref = targets
    load(sources, targets, sems)
    width = s.W * LANES
    pad = s.rows - COMP * s.W
    zeros = jnp.zeros((max(pad, 1), LANES), jnp.float32)
    for i in range(COMP):
        matrix = inverse_ref[i].astype(jnp.float32)
        for o in range(s.W):
            piece = matrix[:, o * LANES : (o + 1) * LANES]
            for h in range(s.H):
                row = h * s.W + o
                spread_out[i, pl.ds(row, SUBLANES, stride=s.index_rows), :] = piece[:SUBLANES]
                row += SUBLANES * s.index_rows
                spread_out[i, row : row + 1, :] = piece[SUBLANES:COMP]
        if pad:
            for f in range(FACES):
                start = (f * COMP + i) * s.rows + COMP * s.W
                coup_out[start : start + pad, :] = zeros
        for j in range(COMP):
            matrix = coupling_ref[i, j].astype(jnp.float32)
            for o in range(s.W):
                coup_out[pl.ds(i * s.rows + j * s.W + o, FACES, stride=COMP * s.rows), :] = matrix[
                    :, o * LANES : (o + 1) * LANES
                ]
    lanes = lax.broadcasted_iota(jnp.int32, (1, LANES), 1)
    for f in range(FACES):
        for o in range(s.W):
            offset = neighbours_ref[f : f + 1, o * LANES : (o + 1) * LANES]
            position = lanes + offset + width
            reach = position >> 7
            tile = reach + o
            inside = (tile >= s.W) & (tile < 2 * s.W)
            wall = offset == 0
            lane = position & (LANES - 1)
            own = jnp.where(wall | ~inside, -1, reach & (s.W - 1))
            halo = jnp.where(wall | inside, -1, jnp.where(tile < s.W, reach, reach - s.W))
            for h in range(s.H):
                row = h * s.W + o
                lane_out[f, row : row + 1, :] = lane
                own_out[f, row : row + 1, :] = own
                halo_out[f, row : row + 1, :] = halo
    even_out[...] = jnp.full((SUBLANES, LANES), 1 - (lax.axis_index(dom) & 1), jnp.int32)


def rows_of(ref, v):
    return ref[v * SUBLANES : (v + 1) * SUBLANES, :]


def times(s, matrix, vectors):
    total = [[None] * s.Q for _ in range(COMP)]
    for i in range(COMP):
        for q in range(s.Q):
            acc = None
            for k, packed in enumerate(vectors):
                for v in range(q, s.NV, s.Q):
                    term = matrix(k, i, v) * packed[v]
                    acc = term if acc is None else acc + term
            total[i][q] = acc
    if s.H == 1:
        return [total[v // s.Q][v % s.Q] for v in range(s.NV)]
    low = lax.broadcasted_iota(jnp.int32, (SUBLANES, LANES), 0) < s.W
    out = []
    for v in range(s.NV):
        a = total[2 * v][0]
        b = total[2 * v + 1][0] if 2 * v + 1 < COMP else jnp.zeros_like(a)
        out.append(jnp.where(low, a, b) + pltpu.roll(jnp.where(low, b, a), s.W, 0))
    return out


def assemble_kernel(s, slots, grp, *refs):
    pieces, out_ref = refs[:-1], refs[-1]
    me = lax.axis_index(grp)
    if s.rows > COMP * s.W:
        out_ref[COMP * s.W :, :] = jnp.zeros((s.rows - COMP * s.W, LANES), jnp.float32)
    for k, piece in enumerate(pieces):
        slot = slots(me, k)
        out_ref[pl.ds(slot, SUBLANES, stride=s.W), :] = piece[:SUBLANES, :]
        out_ref[pl.ds(SUBLANES * s.W + slot, 1), :] = piece[SUBLANES:COMP, :]


def fold_kernel(s, spread_ref, coupling_ref, out_ref):
    group = 3
    for q in range(s.Q):
        pairs = [(f, v) for f in range(FACES) for v in range(q, s.NV, s.Q)]
        for first in range(0, len(pairs), group):
            block = pairs[first : first + group]
            columns = [
                [
                    coupling_ref[(f * COMP + k) * s.rows + v * SUBLANES : (f * COMP + k) * s.rows + (v + 1) * SUBLANES, :]
                    for k in range(COMP)
                ]
                for f, v in block
            ]
            for i in range(COMP):
                acc = [None] * len(block)
                for k in range(COMP):
                    start = k * s.index_rows + q * SUBLANES
                    factor = spread_ref[i, start : start + SUBLANES, :]
                    for n in range(len(block)):
                        term = factor * columns[n][k]
                        acc[n] = term if acc[n] is None else acc[n] + term
                for n, (f, v) in enumerate(block):
                    out_ref[f, i, v * SUBLANES : (v + 1) * SUBLANES, :] = damping * acc[n]


def windows(s, table, low, high):
    if s.H == 1:
        for place, block in ((0, low), (1, high)):
            for v in range(s.NV):
                start = (v // s.Q) * 2 * s.W + place * s.W + (v % s.Q) * SUBLANES
                table[start : start + SUBLANES, :] = block[v]

        def source(v, k):
            start = (v // s.Q) * 2 * s.W + (v % s.Q) * SUBLANES + k
            return table[start : start + SUBLANES, :]

        return source
    top = s.rows + 2 * SUBLANES
    for v in range(s.NV):
        table[v * SUBLANES : (v + 1) * SUBLANES, :] = low[v]
        table[top + v * SUBLANES : top + (v + 1) * SUBLANES, :] = high[v]
    place = place_of_row(s)

    def source(v, k):
        if k == 0:
            return low[v]
        if k == s.W:
            return high[v]
        start = v * SUBLANES + k
        return jnp.where(
            place < s.W - k,
            table[start : start + SUBLANES, :],
            table[top + start - s.W : top + start - s.W + SUBLANES, :],
        )

    return source


def gathered(s, source, count, lane_ref, slot_ref):
    tiles = [[source(v, k) for v in range(s.NV)] for k in range(count)] if s.H > 1 else None
    beside = []
    for f in range(FACES):
        lane = [lane_ref[f, q * SUBLANES : (q + 1) * SUBLANES, :] for q in range(s.Q)]
        slot = [slot_ref[f, q * SUBLANES : (q + 1) * SUBLANES, :] for q in range(s.Q)]
        face = [jnp.zeros((SUBLANES, LANES), jnp.float32)] * s.NV
        for k in range(count):
            here = [slot[q] == k for q in range(s.Q)]
            for v in range(s.NV):
                tile = source(v, k) if tiles is None else tiles[k][v]
                taken = jnp.take_along_axis(tile, lane[v % s.Q], axis=1, mode="promise_in_bounds")
                face[v] = jnp.where(here[v % s.Q], taken, face[v])
        beside.append(face)
    return beside


def own_kernel(s, folded_ref, lane_ref, slot_ref, constant_ref, iterate_ref, out_ref, table):
    own = [rows_of(iterate_ref, v) for v in range(s.NV)]
    beside = gathered(s, windows(s, table, own, own), s.W, lane_ref, slot_ref)
    coupled = times(s, lambda f, i, v: rows_of(folded_ref.at[f, i], v), beside)
    for v in range(s.NV):
        out_ref[v * SUBLANES : (v + 1) * SUBLANES, :] = (
            (1.0 - damping) * own[v] + rows_of(constant_ref, v) - coupled[v]
        )


def with_halo(s, folded_ref, lane_ref, slot_ref, even_ref, base_ref, near_ref, far_ref, table):
    even = even_ref[...] != 0
    near = [rows_of(near_ref, v) for v in range(s.NV)]
    far = [rows_of(far_ref, v) for v in range(s.NV)]
    low = [jnp.where(even, b, a) for a, b in zip(near, far)]
    high = [jnp.where(even, a, b) for a, b in zip(near, far)]
    beside = gathered(s, windows(s, table, low, high), s.W + 1, lane_ref, slot_ref)
    coupled = times(s, lambda f, i, v: rows_of(folded_ref.at[f, i], v), beside)
    return [rows_of(base_ref, v) - coupled[v] for v in range(s.NV)]


def halo_kernel(s, *refs):
    out_ref, table = refs[-2:]
    new = with_halo(s, *refs[:-2], table)
    for v in range(s.NV):
        out_ref[v * SUBLANES : (v + 1) * SUBLANES, :] = new[v]


def last_kernel(s, grp, prolongation_ref, *refs):
    out_ref, table, final = refs[-3:]
    new = with_halo(s, *refs[:-3], table)
    for v in range(s.NV):
        final[v * SUBLANES : (v + 1) * SUBLANES, :] = new[v]
    me = lax.axis_index(grp)
    rows = [final[pl.ds(j * s.W + me, 1), :] for j in range(COMP)]
    for v in range(3):
        acc = None
        for m in range(3):
            term = prolongation_ref[:, m : m + 1] * rows[3 * v + m]
            acc = term if acc is None else acc + term
        out_ref[v] = acc


def f32(*shape):
    return jax.ShapeDtypeStruct(shape, jnp.float32)


def i32(*shape):
    return jax.ShapeDtypeStruct(shape, jnp.int32)


def call(kernel, out_shape, scratch=(), flops=0):
    return pl.pallas_call(
        kernel,
        out_shape=out_shape,
        scratch_shapes=scratch,
        compiler_params=pltpu.CompilerParams(vmem_limit_bytes=16 << 20),
        cost_estimate=pl.CostEstimate(flops=flops, bytes_accessed=0, transcendentals=0),
    )


def call_loading(kernel, out_shape, operands, flops=0):
    return pl.pallas_call(
        kernel,
        out_shape=out_shape,
        in_specs=[pl.BlockSpec(memory_space=pl.ANY)] * len(operands),
        scratch_shapes=[pltpu.VMEM(x.shape, x.dtype) for x in operands]
        + [pltpu.SemaphoreType.DMA((len(operands),))],
        compiler_params=pltpu.CompilerParams(vmem_limit_bytes=16 << 20),
        cost_estimate=pl.CostEstimate(flops=flops, bytes_accessed=0, transcendentals=0),
    )(*[pltpu.with_memory_space_constraint(x, pltpu.MemorySpace.HBM) for x in operands])


def exchanges(n_dom, n_grp):
    out = []
    for first in (0, 1):
        partner = {d: d for d in range(n_dom)}
        for d in range(first, n_dom - 1, 2):
            partner[d], partner[d + 1] = d + 1, d
        perm = []
        for d in range(n_dom):
            for g in range(n_grp):
                to = g ^ 1 if partner[d] == d and n_grp % 2 == 0 else g
                perm.append((d * n_grp + g, partner[d] * n_grp + to))
        out.append(perm)
    return out


def uses_swaps(n_dom, n_grp):
    return n_dom % 2 == 0 and n_grp & (n_grp - 1) == 0 and n_grp <= 4


def swap_order(n_grp):
    return tuple(reversed(range(n_grp)))


def cross_swap(n_dom, n_grp, k):
    return [(d * n_grp + g, (d ^ 1) * n_grp + (g ^ k)) for d in range(n_dom) for g in range(n_grp)]


def cycle(n_dom, n_grp):
    following = {}
    for d in range(n_dom):
        to = d + 2 if d % 2 == 0 else d - 2
        following[d] = to if 0 <= to < n_dom else d ^ 1
    return [(d * n_grp + g, following[d] * n_grp + g) for d in range(n_dom) for g in range(n_grp)]


def local(n_dom, n_grp, fine_level_residual, restriction_matrix, prolongation_matrix, block_inverse, face_coupling, neighbours):
    s = Shape(block_inverse.shape[2])
    element_width = fine_level_residual.shape[2]
    assert element_width == LANES and s.W == n_grp
    hbm = lambda x: pltpu.with_memory_space_constraint(x, pltpu.MemorySpace.HBM)
    own = pl.pallas_call(
        functools.partial(restrict_kernel, "grp"),
        out_shape=f32(COMP, LANES),
        in_specs=[pl.BlockSpec(memory_space=pl.ANY)] * 3,
        scratch_shapes=[
            pltpu.VMEM(fine_level_residual.shape, jnp.float32),
            pltpu.VMEM(restriction_matrix.shape, jnp.float32),
            pltpu.VMEM((COMP, COMP, LANES), block_inverse.dtype),
            pltpu.VMEM((COMP, LANES), jnp.float32),
            pltpu.SemaphoreType.DMA((3,)),
        ],
        compiler_params=pltpu.CompilerParams(vmem_limit_bytes=16 << 20),
        name="restrict",
    )(hbm(fine_level_residual), hbm(restriction_matrix), hbm(block_inverse))
    crossed = uses_swaps(n_dom, n_grp)
    if crossed:
        pieces = [None] * n_grp
        for k in swap_order(n_grp):
            pieces[k] = lax.ppermute(own, ("dom", "grp"), cross_swap(n_dom, n_grp, k))
        slots = lambda me, k: me ^ k
    else:
        all_own = lax.all_gather(own, "grp", axis=0)
        pieces = [all_own[k] for k in range(n_grp)]
        slots = lambda me, k: k
    index = i32(FACES, s.index_rows, LANES)
    spread, coupling, lane, own_slot, halo_slot, even = call_loading(
        functools.partial(prepare_kernel, s, "dom"),
        (
            f32(COMP, COMP * s.index_rows, LANES),
            f32(FACES * COMP * s.rows, LANES),
            index,
            index,
            index,
            i32(SUBLANES, LANES),
        ),
        (block_inverse, jnp.transpose(face_coupling, (1, 2, 0, 3)), neighbours),
        flops=10_000_000,
    )
    folded = call(functools.partial(fold_kernel, s), f32(FACES, COMP, s.rows, LANES), flops=10_000_000)(
        spread, coupling
    )
    block = call(functools.partial(assemble_kernel, s, slots, "grp"), f32(s.rows, LANES))(*pieces)
    table = pltpu.VMEM((s.table_rows, LANES), jnp.float32)
    near_pairs, far_pairs = exchanges(n_dom, n_grp)
    constant = iterate = block
    for index in range(1, SWEEPS):
        swapped = crossed and index == 1
        far = lax.ppermute(iterate, ("dom", "grp"), cycle(n_dom, n_grp) if swapped else far_pairs)
        near = lax.ppermute(iterate, ("dom", "grp"), near_pairs)
        if swapped:
            constant = iterate = near
            near = block
        base = call(
            functools.partial(own_kernel, s), f32(s.rows, LANES), (table,), flops=10_000_000
        )(folded, lane, own_slot, constant, iterate)
        operands = (folded, lane, halo_slot, even, base, near, far)
        if index < SWEEPS - 1:
            iterate = call(functools.partial(halo_kernel, s), f32(s.rows, LANES), (table,))(*operands)
    return call(
        functools.partial(last_kernel, s, "grp"),
        f32(3, prolongation_matrix.shape[0], LANES),
        (table, pltpu.VMEM((s.rows, LANES), jnp.float32)),
    )(prolongation_matrix, *operands)


def solution(mesh):
    placed = (
        P(None, None, ("dom", "grp")),
        P(),
        P(),
        P(None, None, "dom"),
        P(None, None, None, "dom"),
        P(None, "dom"),
    )
    n_dom, n_grp = mesh.shape["dom"], mesh.shape["grp"]
    return jax.shard_map(
        functools.partial(local, n_dom, n_grp),
        mesh=mesh,
        in_specs=placed,
        out_specs=P(None, None, ("dom", "grp")),
        check_vma=False,
    )
```

profile of v0, /device:TPU:1, one launch (start us, length us, event | category | flops | bytes accessed | tf_op | source)
XLA Modules:
  0.0 30.0 jit_solution(10389802997731714661)
XLA Ops:
  0.0 0.9 %restrict.1 = f32[9,128]{1,0:T(8,128)S(1)} custom-call(f32[3,15,128]{2,1,0:T(8,128)} %residual_hbm.1, f32[3,15]{1,0:T(4,128)} %restriction_hbm.1, bf16[9,9,512]{2,1,0:T(8,128)(2,1)} %inverse_hbm.1), custom_call_target="tpu_custom_call" | custom-call | tf_op jit(solution)/shard_map/restrict/pallas_call | solution.py:342
  1.0 0.1 collective-permute-start
  1.0 2.7 %collective-permute-start.1 = (f32[9,128]{1,0:T(8,128)S(1)}, f32[9,128]{1,0:T(8,128)S(1)}, u32[]{:S(2)}, u32[]{:S(2)}) collective-permute-start(f32[9,128]{1,0:T(8,128)S(1)} %restrict.1), channel_id=1, source_target_pairs={{0,5},{1,4},{2,7},{3,6},{4,1},{5,0},{6,3},{7,2},{8,13},{9,12},{10,... | collective-permute-start | bytes 13832 | tf_op jit(solution)/shard_map/ppermute | solution.py:360
  3.7 1.6 %collective-permute-start.2 = (f32[9,128]{1,0:T(8,128)S(1)}, f32[9,128]{1,0:T(8,128)S(1)}, u32[]{:S(2)}, u32[]{:S(2)}) collective-permute-start(f32[9,128]{1,0:T(8,128)S(1)} %restrict.1), channel_id=1, source_target_pairs={{0,6},{1,7},{2,4},{3,5},{4,2},{5,3},{6,0},{7,1},{8,14},{9,15},{10,... | collective-permute-start | bytes 13832 | tf_op jit(solution)/shard_map/ppermute | solution.py:360
  5.2 0.0 collective-permute-start.3
  5.3 0.0 collective-permute-done.refs_0_
  5.3 0.0 collective-permute-done.1.refs_1_
  5.3 1.5 %collective-permute-done.2.refs_2_ = f32[9,128]{1,0:T(8,128)S(1)} collective-permute-done((f32[9,128]{1,0:T(8,128)S(1)}, f32[9,128]{1,0:T(8,128)S(1)}, u32[]{:S(2)}, u32[]{:S(2)}) %collective-permute-start.2) | collective-permute-done | bytes 4640 | tf_op jit(solution)/shard_map/ppermute | solution.py:360
  6.8 2.4 %collective-permute-done.3.refs_3_ = f32[9,128]{1,0:T(8,128)S(1)} collective-permute-done((f32[9,128]{1,0:T(8,128)S(1)}, f32[9,128]{1,0:T(8,128)S(1)}, u32[]{:S(2)}, u32[]{:S(2)}) %collective-permute-start.3) | collective-permute-done | bytes 4640 | tf_op jit(solution)/shard_map/ppermute | solution.py:360
  9.2 0.1 collective-permute-start.4
  9.3 0.4 %collective-permute-start.5 = (f32[40,128]{1,0:T(8,128)S(1)}, f32[40,128]{1,0:T(8,128)S(1)}, u32[]{:S(2)}, u32[]{:S(2)}) collective-permute-start(f32[40,128]{1,0:T(8,128)S(1)} %shard_map.66.refs_5_), channel_id=1, source_target_pairs={{0,8},{1,9},{2,10},{3,11},{4,0},{5,1},{6,2},{7,3},{8,16},{9,17},{1... | collective-permute-start | bytes 61448 | tf_op jit(solution)/shard_map/ppermute | solution.py:389
  9.7 1.3 %shard_map.64 = (f32[9,72,128]{2,1,0:T(8,128)S(1)}, f32[1080,128]{1,0:T(8,128)S(1)}, s32[3,8,128]{2,1,0:T(8,128)S(1)}, s32[3,8,128]{2,1,0:T(8,128)S(1)}, s32[3,8,128]{2,1,0:T(8,128)S(1)}, /*index=5*/s32[8,128]{1,0:T(8,128)S(1)}) custom-call(bf16[9,9,512]{2,1,0:T(8,128)(2,1)} %inverse_hbm.1, bf16[9,9,3,512]{3,2,1,0:T(4,128)(2,1)} %bitcast.1, s32[3,512]{1,0:T(4,128)} %refs_2_.1), custom_call_target="tpu_custom_call" | custom-call | flops 10000000 | tf_op jit(solution)/shard_map/pallas_call | solution.py:291
  11.0 0.4 %shard_map.65.folded_ref.refs_0_ = f32[3,9,40,128]{3,2,1,0:T(8,128)S(1)} custom-call(f32[9,72,128]{2,1,0:T(8,128)S(1)} %get-tuple-element.11.spread_ref, f32[1080,128]{1,0:T(8,128)S(1)} %get-tuple-element.12.coupling_ref), custom_call_target="tpu_custom_call" | custom-call | flops 10000000 | tf_op jit(solution)/shard_map/pallas_call | solution.py:380
  11.4 0.0 collective-permute-done.4.constant_ref.iterate_ref
  11.4 0.1 shard_map.67.refs_4_
  11.5 0.4 %collective-permute-done.5.refs_6_ = f32[40,128]{1,0:T(8,128)S(1)} collective-permute-done((f32[40,128]{1,0:T(8,128)S(1)}, f32[40,128]{1,0:T(8,128)S(1)}, u32[]{:S(2)}, u32[]{:S(2)}) %collective-permute-start.5) | collective-permute-done | bytes 20512 | tf_op jit(solution)/shard_map/ppermute | solution.py:389
  11.9 0.2 shard_map.68.iterate_ref
  12.1 1.3 %collective-permute-start.6 = (f32[40,128]{1,0:T(8,128)S(1)}, f32[40,128]{1,0:T(8,128)S(1)}, u32[]{:S(2)}, u32[]{:S(2)}) collective-permute-start(f32[40,128]{1,0:T(8,128)S(1)} %shard_map.68.iterate_ref), channel_id=1, source_target_pairs={{0,4},{1,5},{2,6},{3,7},{4,0},{5,1},{6,2},{7,3},{8,12},{9,13},{10,... | collective-permute-start | bytes 61448 | tf_op jit(solution)/shard_map/ppermute | solution.py:390
  13.4 1.7 %collective-permute-start.7 = (f32[40,128]{1,0:T(8,128)S(1)}, f32[40,128]{1,0:T(8,128)S(1)}, u32[]{:S(2)}, u32[]{:S(2)}) collective-permute-start(f32[40,128]{1,0:T(8,128)S(1)} %shard_map.68.iterate_ref), channel_id=1, source_target_pairs={{0,1},{1,0},{2,3},{3,2},{4,8},{5,9},{6,10},{7,11},{8,4},{9,5},{10,... | collective-permute-start | bytes 61448 | tf_op jit(solution)/shard_map/ppermute | solution.py:389
  15.0 0.1 shard_map.69.refs_4_
  15.2 0.0 collective-permute-done.6.refs_5_
  15.2 1.6 %collective-permute-done.7.refs_6_ = f32[40,128]{1,0:T(8,128)S(1)} collective-permute-done((f32[40,128]{1,0:T(8,128)S(1)}, f32[40,128]{1,0:T(8,128)S(1)}, u32[]{:S(2)}, u32[]{:S(2)}) %collective-permute-start.7) | collective-permute-done | bytes 20512 | tf_op jit(solution)/shard_map/ppermute | solution.py:389
  16.8 0.2 shard_map.70.iterate_ref
  17.0 0.5 %collective-permute-start.8 = (f32[40,128]{1,0:T(8,128)S(1)}, f32[40,128]{1,0:T(8,128)S(1)}, u32[]{:S(2)}, u32[]{:S(2)}) collective-permute-start(f32[40,128]{1,0:T(8,128)S(1)} %shard_map.70.iterate_ref), channel_id=1, source_target_pairs={{0,4},{1,5},{2,6},{3,7},{4,0},{5,1},{6,2},{7,3},{8,12},{9,13},{10,... | collective-permute-start | bytes 61448 | tf_op jit(solution)/shard_map/ppermute | solution.py:390
  17.5 1.4 %collective-permute-start.9 = (f32[40,128]{1,0:T(8,128)S(1)}, f32[40,128]{1,0:T(8,128)S(1)}, u32[]{:S(2)}, u32[]{:S(2)}) collective-permute-start(f32[40,128]{1,0:T(8,128)S(1)} %shard_map.70.iterate_ref), channel_id=1, source_target_pairs={{0,1},{1,0},{2,3},{3,2},{4,8},{5,9},{6,10},{7,11},{8,4},{9,5},{10,... | collective-permute-start | bytes 61448 | tf_op jit(solution)/shard_map/ppermute | solution.py:389
  18.9 0.1 shard_map.71.refs_4_
  19.1 0.0 collective-permute-done.8.refs_5_
  19.1 1.9 %collective-permute-done.9.refs_6_ = f32[40,128]{1,0:T(8,128)S(1)} collective-permute-done((f32[40,128]{1,0:T(8,128)S(1)}, f32[40,128]{1,0:T(8,128)S(1)}, u32[]{:S(2)}, u32[]{:S(2)}) %collective-permute-start.9) | collective-permute-done | bytes 20512 | tf_op jit(solution)/shard_map/ppermute | solution.py:389
  21.0 0.2 shard_map.72.iterate_ref
  21.1 0.5 %collective-permute-start.10 = (f32[40,128]{1,0:T(8,128)S(1)}, f32[40,128]{1,0:T(8,128)S(1)}, u32[]{:S(2)}, u32[]{:S(2)}) collective-permute-start(f32[40,128]{1,0:T(8,128)S(1)} %shard_map.72.iterate_ref), channel_id=1, source_target_pairs={{0,4},{1,5},{2,6},{3,7},{4,0},{5,1},{6,2},{7,3},{8,12},{9,13},{10,... | collective-permute-start | bytes 61448 | tf_op jit(solution)/shard_map/ppermute | solution.py:390
  21.6 0.9 %collective-permute-start.11 = (f32[40,128]{1,0:T(8,128)S(1)}, f32[40,128]{1,0:T(8,128)S(1)}, u32[]{:S(2)}, u32[]{:S(2)}) collective-permute-start(f32[40,128]{1,0:T(8,128)S(1)} %shard_map.72.iterate_ref), channel_id=1, source_target_pairs={{0,1},{1,0},{2,3},{3,2},{4,8},{5,9},{6,10},{7,11},{8,4},{9,5},{10,... | collective-permute-start | bytes 61448 | tf_op jit(solution)/shard_map/ppermute | solution.py:389
  22.5 0.1 shard_map.73.refs_4_
  22.6 0.0 copy-start
  22.6 0.0 collective-permute-done.10.refs_5_
  22.6 2.5 %collective-permute-done.11.refs_6_ = f32[40,128]{1,0:T(8,128)S(1)} collective-permute-done((f32[40,128]{1,0:T(8,128)S(1)}, f32[40,128]{1,0:T(8,128)S(1)}, u32[]{:S(2)}, u32[]{:S(2)}) %collective-permute-start.11) | collective-permute-done | bytes 20512 | tf_op jit(solution)/shard_map/ppermute | solution.py:389
  25.1 0.2 shard_map.74.iterate_ref
  25.3 0.5 %collective-permute-start.12 = (f32[40,128]{1,0:T(8,128)S(1)}, f32[40,128]{1,0:T(8,128)S(1)}, u32[]{:S(2)}, u32[]{:S(2)}) collective-permute-start(f32[40,128]{1,0:T(8,128)S(1)} %shard_map.74.iterate_ref), channel_id=1, source_target_pairs={{0,4},{1,5},{2,6},{3,7},{4,0},{5,1},{6,2},{7,3},{8,12},{9,13},{10,... | collective-permute-start | bytes 61448 | tf_op jit(solution)/shard_map/ppermute | solution.py:390
  25.7 0.6 %collective-permute-start.13 = (f32[40,128]{1,0:T(8,128)S(1)}, f32[40,128]{1,0:T(8,128)S(1)}, u32[]{:S(2)}, u32[]{:S(2)}) collective-permute-start(f32[40,128]{1,0:T(8,128)S(1)} %shard_map.74.iterate_ref), channel_id=1, source_target_pairs={{0,1},{1,0},{2,3},{3,2},{4,8},{5,9},{6,10},{7,11},{8,4},{9,5},{10,... | collective-permute-start | bytes 61448 | tf_op jit(solution)/shard_map/ppermute | solution.py:389
  26.3 0.0 copy-done
  26.3 0.1 copy.7.prolongation_ref
  26.4 0.1 shard_map.75.refs_4_
  26.5 0.0 collective-permute-done.12.refs_5_
  26.6 2.7 %collective-permute-done.13.refs_6_ = f32[40,128]{1,0:T(8,128)S(1)} collective-permute-done((f32[40,128]{1,0:T(8,128)S(1)}, f32[40,128]{1,0:T(8,128)S(1)}, u32[]{:S(2)}, u32[]{:S(2)}) %collective-permute-start.13) | collective-permute-done | bytes 20512 | tf_op jit(solution)/shard_map/ppermute | solution.py:389
  29.2 0.8 %shard_map.76 = f32[3,15,128]{2,1,0:T(8,128)} custom-call(f32[15,3]{1,0:T(8,128)S(1)} %copy.7.prolongation_ref, f32[3,9,40,128]{3,2,1,0:T(8,128)S(1)} %shard_map.65.folded_ref.refs_0_, s32[3,8,128]{2,1,0:T(8,128)S(1)} %get-tuple-element.13.lane_ref.refs_1_, s32[3,8,128]{2,1,0:T(8,128)S(1)} %get-tuple-element.14.refs_2_, ...), custom_call_target="tpu_custom_call" | custom-call | tf_op jit(solution)/shard_map/pallas_call | solution.py:400
  (1 shorter events, 0.0 us)
Async XLA Ops:
  1.0 4.3 %collective-permute-start = (f32[9,128]{1,0:T(8,128)S(1)}, f32[9,128]{1,0:T(8,128)S(1)}, u32[]{:S(2)}, u32[]{:S(2)}) collective-permute-start(f32[9,128]{1,0:T(8,128)S(1)} %restrict.1), channel_id=1, source_target_pairs={{0,4},{1,5},{2,6},{3,7},{4,0},{5,1},{6,2},{7,3},{8,12},{9,13},{10,... | collective-permute-start | bytes 13832 | tf_op jit(solution)/shard_map/ppermute | solution.py:360
  1.0 4.2 %collective-permute-start.1 = (f32[9,128]{1,0:T(8,128)S(1)}, f32[9,128]{1,0:T(8,128)S(1)}, u32[]{:S(2)}, u32[]{:S(2)}) collective-permute-start(f32[9,128]{1,0:T(8,128)S(1)} %restrict.1), channel_id=1, source_target_pairs={{0,5},{1,4},{2,7},{3,6},{4,1},{5,0},{6,3},{7,2},{8,13},{9,12},{10,... | collective-permute-start | bytes 13832 | tf_op jit(solution)/shard_map/ppermute | solution.py:360
  3.7 3.1 %collective-permute-start.2 = (f32[9,128]{1,0:T(8,128)S(1)}, f32[9,128]{1,0:T(8,128)S(1)}, u32[]{:S(2)}, u32[]{:S(2)}) collective-permute-start(f32[9,128]{1,0:T(8,128)S(1)} %restrict.1), channel_id=1, source_target_pairs={{0,6},{1,7},{2,4},{3,5},{4,2},{5,3},{6,0},{7,1},{8,14},{9,15},{10,... | collective-permute-start | bytes 13832 | tf_op jit(solution)/shard_map/ppermute | solution.py:360
  5.2 4.0 %collective-permute-start.3 = (f32[9,128]{1,0:T(8,128)S(1)}, f32[9,128]{1,0:T(8,128)S(1)}, u32[]{:S(2)}, u32[]{:S(2)}) collective-permute-start(f32[9,128]{1,0:T(8,128)S(1)} %restrict.1), channel_id=1, source_target_pairs={{0,7},{1,6},{2,5},{3,4},{4,3},{5,2},{6,1},{7,0},{8,15},{9,14},{10,... | collective-permute-start | bytes 13832 | tf_op jit(solution)/shard_map/ppermute | solution.py:360
  9.2 2.1 %collective-permute-start.4 = (f32[40,128]{1,0:T(8,128)S(1)}, f32[40,128]{1,0:T(8,128)S(1)}, u32[]{:S(2)}, u32[]{:S(2)}) collective-permute-start(f32[40,128]{1,0:T(8,128)S(1)} %shard_map.66.refs_5_), channel_id=1, source_target_pairs={{0,4},{1,5},{2,6},{3,7},{4,0},{5,1},{6,2},{7,3},{8,12},{9,13},{10,... | collective-permute-start | bytes 61448 | tf_op jit(solution)/shard_map/ppermute | solution.py:390
  9.3 2.6 %collective-permute-start.5 = (f32[40,128]{1,0:T(8,128)S(1)}, f32[40,128]{1,0:T(8,128)S(1)}, u32[]{:S(2)}, u32[]{:S(2)}) collective-permute-start(f32[40,128]{1,0:T(8,128)S(1)} %shard_map.66.refs_5_), channel_id=1, source_target_pairs={{0,8},{1,9},{2,10},{3,11},{4,0},{5,1},{6,2},{7,3},{8,16},{9,17},{1... | collective-permute-start | bytes 61448 | tf_op jit(solution)/shard_map/ppermute | solution.py:389
  12.1 3.1 %collective-permute-start.6 = (f32[40,128]{1,0:T(8,128)S(1)}, f32[40,128]{1,0:T(8,128)S(1)}, u32[]{:S(2)}, u32[]{:S(2)}) collective-permute-start(f32[40,128]{1,0:T(8,128)S(1)} %shard_map.68.iterate_ref), channel_id=1, source_target_pairs={{0,4},{1,5},{2,6},{3,7},{4,0},{5,1},{6,2},{7,3},{8,12},{9,13},{10,... | collective-permute-start | bytes 61448 | tf_op jit(solution)/shard_map/ppermute | solution.py:390
  13.4 3.5 %collective-permute-start.7 = (f32[40,128]{1,0:T(8,128)S(1)}, f32[40,128]{1,0:T(8,128)S(1)}, u32[]{:S(2)}, u32[]{:S(2)}) collective-permute-start(f32[40,128]{1,0:T(8,128)S(1)} %shard_map.68.iterate_ref), channel_id=1, source_target_pairs={{0,1},{1,0},{2,3},{3,2},{4,8},{5,9},{6,10},{7,11},{8,4},{9,5},{10,... | collective-permute-start | bytes 61448 | tf_op jit(solution)/shard_map/ppermute | solution.py:389
  17.0 2.1 %collective-permute-start.8 = (f32[40,128]{1,0:T(8,128)S(1)}, f32[40,128]{1,0:T(8,128)S(1)}, u32[]{:S(2)}, u32[]{:S(2)}) collective-permute-start(f32[40,128]{1,0:T(8,128)S(1)} %shard_map.70.iterate_ref), channel_id=1, source_target_pairs={{0,4},{1,5},{2,6},{3,7},{4,0},{5,1},{6,2},{7,3},{8,12},{9,13},{10,... | collective-permute-start | bytes 61448 | tf_op jit(solution)/shard_map/ppermute | solution.py:390
  17.5 3.5 %collective-permute-start.9 = (f32[40,128]{1,0:T(8,128)S(1)}, f32[40,128]{1,0:T(8,128)S(1)}, u32[]{:S(2)}, u32[]{:S(2)}) collective-permute-start(f32[40,128]{1,0:T(8,128)S(1)} %shard_map.70.iterate_ref), channel_id=1, source_target_pairs={{0,1},{1,0},{2,3},{3,2},{4,8},{5,9},{6,10},{7,11},{8,4},{9,5},{10,... | collective-permute-start | bytes 61448 | tf_op jit(solution)/shard_map/ppermute | solution.py:389
  21.1 1.5 %collective-permute-start.10 = (f32[40,128]{1,0:T(8,128)S(1)}, f32[40,128]{1,0:T(8,128)S(1)}, u32[]{:S(2)}, u32[]{:S(2)}) collective-permute-start(f32[40,128]{1,0:T(8,128)S(1)} %shard_map.72.iterate_ref), channel_id=1, source_target_pairs={{0,4},{1,5},{2,6},{3,7},{4,0},{5,1},{6,2},{7,3},{8,12},{9,13},{10,... | collective-permute-start | bytes 61448 | tf_op jit(solution)/shard_map/ppermute | solution.py:390
  21.6 3.5 %collective-permute-start.11 = (f32[40,128]{1,0:T(8,128)S(1)}, f32[40,128]{1,0:T(8,128)S(1)}, u32[]{:S(2)}, u32[]{:S(2)}) collective-permute-start(f32[40,128]{1,0:T(8,128)S(1)} %shard_map.72.iterate_ref), channel_id=1, source_target_pairs={{0,1},{1,0},{2,3},{3,2},{4,8},{5,9},{6,10},{7,11},{8,4},{9,5},{10,... | collective-permute-start | bytes 61448 | tf_op jit(solution)/shard_map/ppermute | solution.py:389
  22.6 3.7 %copy-start = (f32[15,3]{0,1:T(4,128)S(1)}, f32[15,3]{0,1:T(4,128)}, u32[]{:S(2)}) copy-start(f32[15,3]{0,1:T(4,128)} %param.8) | copy-start | bytes 544
  25.3 1.3 %collective-permute-start.12 = (f32[40,128]{1,0:T(8,128)S(1)}, f32[40,128]{1,0:T(8,128)S(1)}, u32[]{:S(2)}, u32[]{:S(2)}) collective-permute-start(f32[40,128]{1,0:T(8,128)S(1)} %shard_map.74.iterate_ref), channel_id=1, source_target_pairs={{0,4},{1,5},{2,6},{3,7},{4,0},{5,1},{6,2},{7,3},{8,12},{9,13},{10,... | collective-permute-start | bytes 61448 | tf_op jit(solution)/shard_map/ppermute | solution.py:390
  25.7 3.5 %collective-permute-start.13 = (f32[40,128]{1,0:T(8,128)S(1)}, f32[40,128]{1,0:T(8,128)S(1)}, u32[]{:S(2)}, u32[]{:S(2)}) collective-permute-start(f32[40,128]{1,0:T(8,128)S(1)} %shard_map.74.iterate_ref), channel_id=1, source_target_pairs={{0,1},{1,0},{2,3},{3,2},{4,8},{5,9},{6,10},{7,11},{8,4},{9,5},{10,... | collective-permute-start | bytes 61448 | tf_op jit(solution)/shard_map/ppermute | solution.py:389
where the time goes:
time: 30.6 us; the launch traced here: 30 us
  waiting for transfers between devices  13.1 us (43%)
  starting transfers between devices  11.9 us (39%)
  Pallas kernels  4.76 us (16%)
    ppermute x5, waiting for transfers between devices, local(): lax.ppermute(iterate, ('dom', 'grp'), cycle(n_dom, n_grp) if swapped else...  9.07 us
    ppermute x5, starting transfers between devices, local(): lax.ppermute(iterate, ('dom', 'grp'), cycle(n_dom, n_grp) if swapped else...  4.94 us
    ppermute x4, starting transfers between devices, local(): pieces[k] = lax.ppermute(own, ('dom', 'grp'), cross_swap(n_dom, n_grp, k))  4.29 us
    ppermute x4, waiting for transfers between devices, local(): pieces[k] = lax.ppermute(own, ('dom', 'grp'), cross_swap(n_dom, n_grp, k))  3.97 us
    ppermute x5, starting transfers between devices, local(): near = lax.ppermute(iterate, ('dom', 'grp'), near_pairs)  2.71 us
    pallas_call x1, Pallas kernels, call_loading(): pl.pallas_call(kernel, out_shape=out_shape, in_specs=[pl.BlockSpec(memory...  1.27 us
    pallas_call x1, Pallas kernels, local(): pl.pallas_call(functools.partial(restrict_kernel, 'grp'), out_shape=f32(C...  0.95 us
    pallas_call x1, Pallas kernels, local(): call(functools.partial(last_kernel, s, 'grp'), f32(3, prolongation_matrix...  0.8 us
  transfers between devices with their start and end apart: 14, of which 7 were waited for; matrix products, arithmetic and copies ran while one was open for 0% of the time, Pallas kernels for 8%

commit v1 on v0

--- a/solution.py
+++ b/solution.py
@@ -45,11 +45,9 @@
 
 def restrict_kernel(grp, residual_hbm, restriction_hbm, inverse_hbm, out_ref, residual_ref, restriction_ref, inverse_ref, rhs_ref, sems):
     columns = pl.ds(pl.multiple_of(lax.axis_index(grp) * LANES, LANES), LANES)
-    load(
-        (residual_hbm, restriction_hbm, inverse_hbm.at[:, :, columns]),
-        (residual_ref, restriction_ref, inverse_ref),
-        sems,
-    )
+    inverse_copy = pltpu.make_async_copy(inverse_hbm.at[:, :, columns], inverse_ref, sems.at[2])
+    inverse_copy.start()
+    load((residual_hbm, restriction_hbm), (residual_ref, restriction_ref), sems)
     nodes = residual_ref.shape[1]
     diagonal = lax.broadcasted_iota(jnp.int32, (nodes, nodes), 0) == lax.broadcasted_iota(
         jnp.int32, (nodes, nodes), 1
@@ -62,6 +60,7 @@
                 column * residual_ref[v], axis=0, keepdims=True
             )
     rhs = rhs_ref[...]
+    inverse_copy.wait()
     for i in range(COMP):
         out_ref[i : i + 1, :] = damping * jnp.sum(
             inverse_ref[i].astype(jnp.float32) * rhs, axis=0, keepdims=True
@@ -299,7 +298,7 @@
     )(*[pltpu.with_memory_space_constraint(x, pltpu.MemorySpace.HBM) for x in operands])
 
 
-def exchanges(n_dom, n_grp):
+def exchanges(n_dom, n_grp, fill):
     out = []
     for first in (0, 1):
         partner = {d: d for d in range(n_dom)}
@@ -309,7 +308,8 @@
         for d in range(n_dom):
             for g in range(n_grp):
                 to = g ^ 1 if partner[d] == d and n_grp % 2 == 0 else g
-                perm.append((d * n_grp + g, partner[d] * n_grp + to))
+                if fill or partner[d] != d:
+                    perm.append((d * n_grp + g, partner[d] * n_grp + to))
         out.append(perm)
     return out
 
@@ -319,7 +319,7 @@
 
 
 def swap_order(n_grp):
-    return tuple(reversed(range(n_grp)))
+    return (*range(n_grp - 1, n_grp // 2, -1), *range(1, n_grp // 2 + 1), 0)
 
 
 def cross_swap(n_dom, n_grp, k):
@@ -382,10 +382,10 @@
     )
     block = call(functools.partial(assemble_kernel, s, slots, "grp"), f32(s.rows, LANES))(*pieces)
     table = pltpu.VMEM((s.table_rows, LANES), jnp.float32)
-    near_pairs, far_pairs = exchanges(n_dom, n_grp)
     constant = iterate = block
     for index in range(1, SWEEPS):
         swapped = crossed and index == 1
+        near_pairs, far_pairs = exchanges(n_dom, n_grp, index < SWEEPS - 1)
         far = lax.ppermute(iterate, ("dom", "grp"), cycle(n_dom, n_grp) if swapped else far_pairs)
         near = lax.ppermute(iterate, ("dom", "grp"), near_pairs)
         if swapped:

time: 30.6 us -> 31.8 us (1.039); the launches traced: 30 us -> 31.6 us
  starting transfers between devices: 11.9 us -> 13.8 us
  waiting for transfers between devices: 13.1 us -> 12.7 us
    ppermute x5, starting transfers between devices: 4.94 us -> 6.84 us  [local(): lax.ppermute(iterate, ('dom', 'grp'), cycle(n_dom, n_grp) if swapped else...]
  transfers between devices with their start and end apart: 14 -> 14, of which waited for: 7 -> 7; matrix products, arithmetic and copies ran while one was open for 0% -> 0% of each run, Pallas kernels for 8% -> 7%
where the time goes in v1:
time: 31.8 us; the launch traced here: 31.6 us
  starting transfers between devices  13.8 us (43%)
  waiting for transfers between devices  12.7 us (40%)
  Pallas kernels  4.73 us (15%)
    ppermute x5, waiting for transfers between devices, local(): lax.ppermute(iterate, ('dom', 'grp'), cycle(n_dom, n_grp) if swapped else...  8.76 us
    ppermute x5, starting transfers between devices, local(): lax.ppermute(iterate, ('dom', 'grp'), cycle(n_dom, n_grp) if swapped else...  6.84 us
    ppermute x4, starting transfers between devices, local(): pieces[k] = lax.ppermute(own, ('dom', 'grp'), cross_swap(n_dom, n_grp, k))  4.29 us
    ppermute x4, waiting for transfers between devices, local(): pieces[k] = lax.ppermute(own, ('dom', 'grp'), cross_swap(n_dom, n_grp, k))  3.97 us
    ppermute x5, starting transfers between devices, local(): near = lax.ppermute(iterate, ('dom', 'grp'), near_pairs)  2.71 us
    pallas_call x1, Pallas kernels, call_loading(): pl.pallas_call(kernel, out_shape=out_shape, in_specs=[pl.BlockSpec(memory...  1.27 us
    pallas_call x1, Pallas kernels, local(): pl.pallas_call(functools.partial(restrict_kernel, 'grp'), out_shape=f32(C...  0.91 us
    pallas_call x1, Pallas kernels, local(): call(functools.partial(last_kernel, s, 'grp'), f32(3, prolongation_matrix...  0.8 us
  transfers between devices with their start and end apart: 14, of which 7 were waited for; matrix products, arithmetic and copies ran while one was open for 0% of the time, Pallas kernels for 7%

profile of v1, /device:TPU:1, one launch (start us, length us, event | category | flops | bytes accessed | tf_op | source)
XLA Modules:
  0.0 31.6 jit_solution(18018072293672463152)
XLA Ops:
  0.0 0.9 %restrict.1 = f32[9,128]{1,0:T(8,128)S(1)} custom-call(f32[3,15,128]{2,1,0:T(8,128)} %residual_hbm.1, f32[3,15]{1,0:T(4,128)} %restriction_hbm.1, bf16[9,9,512]{2,1,0:T(8,128)(2,1)} %inverse_hbm.1), custom_call_target="tpu_custom_call" | custom-call | tf_op jit(solution)/shard_map/restrict/pallas_call | solution.py:342
  0.9 0.1 collective-permute-start
  1.0 2.7 %collective-permute-start.1 = (f32[9,128]{1,0:T(8,128)S(1)}, f32[9,128]{1,0:T(8,128)S(1)}, u32[]{:S(2)}, u32[]{:S(2)}) collective-permute-start(f32[9,128]{1,0:T(8,128)S(1)} %restrict.1), channel_id=1, source_target_pairs={{0,5},{1,4},{2,7},{3,6},{4,1},{5,0},{6,3},{7,2},{8,13},{9,12},{10,... | collective-permute-start | bytes 13832 | tf_op jit(solution)/shard_map/ppermute | solution.py:360
  3.7 1.6 %collective-permute-start.2 = (f32[9,128]{1,0:T(8,128)S(1)}, f32[9,128]{1,0:T(8,128)S(1)}, u32[]{:S(2)}, u32[]{:S(2)}) collective-permute-start(f32[9,128]{1,0:T(8,128)S(1)} %restrict.1), channel_id=1, source_target_pairs={{0,6},{1,7},{2,4},{3,5},{4,2},{5,3},{6,0},{7,1},{8,14},{9,15},{10,... | collective-permute-start | bytes 13832 | tf_op jit(solution)/shard_map/ppermute | solution.py:360
  5.2 0.0 collective-permute-start.3
  5.2 0.0 collective-permute-done.refs_0_
  5.2 0.0 collective-permute-done.1.refs_1_
  5.2 1.5 %collective-permute-done.2.refs_2_ = f32[9,128]{1,0:T(8,128)S(1)} collective-permute-done((f32[9,128]{1,0:T(8,128)S(1)}, f32[9,128]{1,0:T(8,128)S(1)}, u32[]{:S(2)}, u32[]{:S(2)}) %collective-permute-start.2) | collective-permute-done | bytes 4640 | tf_op jit(solution)/shard_map/ppermute | solution.py:360
  6.8 2.4 %collective-permute-done.3.refs_3_ = f32[9,128]{1,0:T(8,128)S(1)} collective-permute-done((f32[9,128]{1,0:T(8,128)S(1)}, f32[9,128]{1,0:T(8,128)S(1)}, u32[]{:S(2)}, u32[]{:S(2)}) %collective-permute-start.3) | collective-permute-done | bytes 4640 | tf_op jit(solution)/shard_map/ppermute | solution.py:360
  9.2 0.1 collective-permute-start.4
  9.3 0.4 %collective-permute-start.5 = (f32[40,128]{1,0:T(8,128)S(1)}, f32[40,128]{1,0:T(8,128)S(1)}, u32[]{:S(2)}, u32[]{:S(2)}) collective-permute-start(f32[40,128]{1,0:T(8,128)S(1)} %shard_map.66.refs_5_), channel_id=1, source_target_pairs={{0,8},{1,9},{2,10},{3,11},{4,0},{5,1},{6,2},{7,3},{8,16},{9,17},{1... | collective-permute-start | bytes 61448 | tf_op jit(solution)/shard_map/ppermute | solution.py:389
  9.7 1.3 %shard_map.64 = (f32[9,72,128]{2,1,0:T(8,128)S(1)}, f32[1080,128]{1,0:T(8,128)S(1)}, s32[3,8,128]{2,1,0:T(8,128)S(1)}, s32[3,8,128]{2,1,0:T(8,128)S(1)}, s32[3,8,128]{2,1,0:T(8,128)S(1)}, /*index=5*/s32[8,128]{1,0:T(8,128)S(1)}) custom-call(bf16[9,9,512]{2,1,0:T(8,128)(2,1)} %inverse_hbm.1, bf16[9,9,3,512]{3,2,1,0:T(4,128)(2,1)} %bitcast.1, s32[3,512]{1,0:T(4,128)} %refs_2_.1), custom_call_target="tpu_custom_call" | custom-call | flops 10000000 | tf_op jit(solution)/shard_map/pallas_call | solution.py:290
  11.0 0.4 %shard_map.65.folded_ref.refs_0_ = f32[3,9,40,128]{3,2,1,0:T(8,128)S(1)} custom-call(f32[9,72,128]{2,1,0:T(8,128)S(1)} %get-tuple-element.11.spread_ref, f32[1080,128]{1,0:T(8,128)S(1)} %get-tuple-element.12.coupling_ref), custom_call_target="tpu_custom_call" | custom-call | flops 10000000 | tf_op jit(solution)/shard_map/pallas_call | solution.py:380
  11.3 0.0 collective-permute-done.4.constant_ref.iterate_ref
  11.3 0.1 shard_map.67.refs_4_
  11.5 0.4 %collective-permute-done.5.refs_6_ = f32[40,128]{1,0:T(8,128)S(1)} collective-permute-done((f32[40,128]{1,0:T(8,128)S(1)}, f32[40,128]{1,0:T(8,128)S(1)}, u32[]{:S(2)}, u32[]{:S(2)}) %collective-permute-start.5) | collective-permute-done | bytes 20512 | tf_op jit(solution)/shard_map/ppermute | solution.py:389
  11.9 0.2 shard_map.68.iterate_ref
  12.1 1.3 %collective-permute-start.6 = (f32[40,128]{1,0:T(8,128)S(1)}, f32[40,128]{1,0:T(8,128)S(1)}, u32[]{:S(2)}, u32[]{:S(2)}) collective-permute-start(f32[40,128]{1,0:T(8,128)S(1)} %shard_map.68.iterate_ref), channel_id=1, source_target_pairs={{0,4},{1,5},{2,6},{3,7},{4,0},{5,1},{6,2},{7,3},{8,12},{9,13},{10,... | collective-permute-start | bytes 61448 | tf_op jit(solution)/shard_map/ppermute | solution.py:390
  13.3 1.7 %collective-permute-start.7 = (f32[40,128]{1,0:T(8,128)S(1)}, f32[40,128]{1,0:T(8,128)S(1)}, u32[]{:S(2)}, u32[]{:S(2)}) collective-permute-start(f32[40,128]{1,0:T(8,128)S(1)} %shard_map.68.iterate_ref), channel_id=1, source_target_pairs={{0,1},{1,0},{2,3},{3,2},{4,8},{5,9},{6,10},{7,11},{8,4},{9,5},{10,... | collective-permute-start | bytes 61448 | tf_op jit(solution)/shard_map/ppermute | solution.py:389
  15.0 0.1 shard_map.69.refs_4_
  15.1 0.0 collective-permute-done.6.refs_5_
  15.1 1.6 %collective-permute-done.7.refs_6_ = f32[40,128]{1,0:T(8,128)S(1)} collective-permute-done((f32[40,128]{1,0:T(8,128)S(1)}, f32[40,128]{1,0:T(8,128)S(1)}, u32[]{:S(2)}, u32[]{:S(2)}) %collective-permute-start.7) | collective-permute-done | bytes 20512 | tf_op jit(solution)/shard_map/ppermute | solution.py:389
  16.8 0.2 shard_map.70.iterate_ref
  17.0 0.5 %collective-permute-start.8 = (f32[40,128]{1,0:T(8,128)S(1)}, f32[40,128]{1,0:T(8,128)S(1)}, u32[]{:S(2)}, u32[]{:S(2)}) collective-permute-start(f32[40,128]{1,0:T(8,128)S(1)} %shard_map.70.iterate_ref), channel_id=1, source_target_pairs={{0,4},{1,5},{2,6},{3,7},{4,0},{5,1},{6,2},{7,3},{8,12},{9,13},{10,... | collective-permute-start | bytes 61448 | tf_op jit(solution)/shard_map/ppermute | solution.py:390
  17.4 1.4 %collective-permute-start.9 = (f32[40,128]{1,0:T(8,128)S(1)}, f32[40,128]{1,0:T(8,128)S(1)}, u32[]{:S(2)}, u32[]{:S(2)}) collective-permute-start(f32[40,128]{1,0:T(8,128)S(1)} %shard_map.70.iterate_ref), channel_id=1, source_target_pairs={{0,1},{1,0},{2,3},{3,2},{4,8},{5,9},{6,10},{7,11},{8,4},{9,5},{10,... | collective-permute-start | bytes 61448 | tf_op jit(solution)/shard_map/ppermute | solution.py:389
  18.9 0.1 shard_map.71.refs_4_
  19.0 0.0 collective-permute-done.8.refs_5_
  19.0 1.9 %collective-permute-done.9.refs_6_ = f32[40,128]{1,0:T(8,128)S(1)} collective-permute-done((f32[40,128]{1,0:T(8,128)S(1)}, f32[40,128]{1,0:T(8,128)S(1)}, u32[]{:S(2)}, u32[]{:S(2)}) %collective-permute-start.9) | collective-permute-done | bytes 20512 | tf_op jit(solution)/shard_map/ppermute | solution.py:389
  20.9 0.2 shard_map.72.iterate_ref
  21.1 0.5 %collective-permute-start.10 = (f32[40,128]{1,0:T(8,128)S(1)}, f32[40,128]{1,0:T(8,128)S(1)}, u32[]{:S(2)}, u32[]{:S(2)}) collective-permute-start(f32[40,128]{1,0:T(8,128)S(1)} %shard_map.72.iterate_ref), channel_id=1, source_target_pairs={{0,4},{1,5},{2,6},{3,7},{4,0},{5,1},{6,2},{7,3},{8,12},{9,13},{10,... | collective-permute-start | bytes 61448 | tf_op jit(solution)/shard_map/ppermute | solution.py:390
  21.6 0.9 %collective-permute-start.11 = (f32[40,128]{1,0:T(8,128)S(1)}, f32[40,128]{1,0:T(8,128)S(1)}, u32[]{:S(2)}, u32[]{:S(2)}) collective-permute-start(f32[40,128]{1,0:T(8,128)S(1)} %shard_map.72.iterate_ref), channel_id=1, source_target_pairs={{0,1},{1,0},{2,3},{3,2},{4,8},{5,9},{6,10},{7,11},{8,4},{9,5},{10,... | collective-permute-start | bytes 61448 | tf_op jit(solution)/shard_map/ppermute | solution.py:389
  22.4 0.1 shard_map.73.refs_4_
  22.6 0.0 copy-start
  22.6 0.0 collective-permute-done.10.refs_5_
  22.6 2.5 %collective-permute-done.11.refs_6_ = f32[40,128]{1,0:T(8,128)S(1)} collective-permute-done((f32[40,128]{1,0:T(8,128)S(1)}, f32[40,128]{1,0:T(8,128)S(1)}, u32[]{:S(2)}, u32[]{:S(2)}) %collective-permute-start.11) | collective-permute-done | bytes 20512 | tf_op jit(solution)/shard_map/ppermute | solution.py:389
  25.1 0.2 shard_map.74.iterate_ref
  25.2 0.5 %collective-permute-start.12 = (f32[40,128]{1,0:T(8,128)S(1)}, f32[40,128]{1,0:T(8,128)S(1)}, u32[]{:S(2)}, u32[]{:S(2)}) collective-permute-start(f32[40,128]{1,0:T(8,128)S(1)} %shard_map.74.iterate_ref), channel_id=1, source_target_pairs={{0,4},{1,5},{2,6},{3,7},{4,0},{5,1},{6,2},{7,3},{8,12},{9,13},{10,... | collective-permute-start | bytes 61448 | tf_op jit(solution)/shard_map/ppermute | solution.py:390
  25.7 2.5 %collective-permute-start.13 = (f32[40,128]{1,0:T(8,128)S(1)}, f32[40,128]{1,0:T(8,128)S(1)}, u32[]{:S(2)}, u32[]{:S(2)}) collective-permute-start(f32[40,128]{1,0:T(8,128)S(1)} %shard_map.74.iterate_ref), channel_id=1, source_target_pairs={{4,8},{5,9},{6,10},{7,11},{8,4},{9,5},{10,6},{11,7},{12,16},{13,17... | collective-permute-start | bytes 61448 | tf_op jit(solution)/shard_map/ppermute | solution.py:389
  28.2 0.0 copy-done
  28.2 0.1 copy.7.prolongation_ref
  28.3 0.1 shard_map.75.refs_4_
  28.4 0.0 collective-permute-done.12.refs_5_
  28.4 2.3 %collective-permute-done.13.refs_6_ = f32[40,128]{1,0:T(8,128)S(1)} collective-permute-done((f32[40,128]{1,0:T(8,128)S(1)}, f32[40,128]{1,0:T(8,128)S(1)}, u32[]{:S(2)}, u32[]{:S(2)}) %collective-permute-start.13) | collective-permute-done | bytes 20512 | tf_op jit(solution)/shard_map/ppermute | solution.py:389
  30.8 0.8 %shard_map.76 = f32[3,15,128]{2,1,0:T(8,128)} custom-call(f32[15,3]{1,0:T(8,128)S(1)} %copy.7.prolongation_ref, f32[3,9,40,128]{3,2,1,0:T(8,128)S(1)} %shard_map.65.folded_ref.refs_0_, s32[3,8,128]{2,1,0:T(8,128)S(1)} %get-tuple-element.13.lane_ref.refs_1_, s32[3,8,128]{2,1,0:T(8,128)S(1)} %get-tuple-element.14.refs_2_, ...), custom_call_target="tpu_custom_call" | custom-call | tf_op jit(solution)/shard_map/pallas_call | solution.py:400
  (1 shorter events, 0.0 us)
Async XLA Ops:
  0.9 4.3 %collective-permute-start = (f32[9,128]{1,0:T(8,128)S(1)}, f32[9,128]{1,0:T(8,128)S(1)}, u32[]{:S(2)}, u32[]{:S(2)}) collective-permute-start(f32[9,128]{1,0:T(8,128)S(1)} %restrict.1), channel_id=1, source_target_pairs={{0,4},{1,5},{2,6},{3,7},{4,0},{5,1},{6,2},{7,3},{8,12},{9,13},{10,... | collective-permute-start | bytes 13832 | tf_op jit(solution)/shard_map/ppermute | solution.py:360
  1.0 4.2 %collective-permute-start.1 = (f32[9,128]{1,0:T(8,128)S(1)}, f32[9,128]{1,0:T(8,128)S(1)}, u32[]{:S(2)}, u32[]{:S(2)}) collective-permute-start(f32[9,128]{1,0:T(8,128)S(1)} %restrict.1), channel_id=1, source_target_pairs={{0,5},{1,4},{2,7},{3,6},{4,1},{5,0},{6,3},{7,2},{8,13},{9,12},{10,... | collective-permute-start | bytes 13832 | tf_op jit(solution)/shard_map/ppermute | solution.py:360
  3.7 3.1 %collective-permute-start.2 = (f32[9,128]{1,0:T(8,128)S(1)}, f32[9,128]{1,0:T(8,128)S(1)}, u32[]{:S(2)}, u32[]{:S(2)}) collective-permute-start(f32[9,128]{1,0:T(8,128)S(1)} %restrict.1), channel_id=1, source_target_pairs={{0,6},{1,7},{2,4},{3,5},{4,2},{5,3},{6,0},{7,1},{8,14},{9,15},{10,... | collective-permute-start | bytes 13832 | tf_op jit(solution)/shard_map/ppermute | solution.py:360
  5.2 4.0 %collective-permute-start.3 = (f32[9,128]{1,0:T(8,128)S(1)}, f32[9,128]{1,0:T(8,128)S(1)}, u32[]{:S(2)}, u32[]{:S(2)}) collective-permute-start(f32[9,128]{1,0:T(8,128)S(1)} %restrict.1), channel_id=1, source_target_pairs={{0,7},{1,6},{2,5},{3,4},{4,3},{5,2},{6,1},{7,0},{8,15},{9,14},{10,... | collective-permute-start | bytes 13832 | tf_op jit(solution)/shard_map/ppermute | solution.py:360
  9.2 2.1 %collective-permute-start.4 = (f32[40,128]{1,0:T(8,128)S(1)}, f32[40,128]{1,0:T(8,128)S(1)}, u32[]{:S(2)}, u32[]{:S(2)}) collective-permute-start(f32[40,128]{1,0:T(8,128)S(1)} %shard_map.66.refs_5_), channel_id=1, source_target_pairs={{0,4},{1,5},{2,6},{3,7},{4,0},{5,1},{6,2},{7,3},{8,12},{9,13},{10,... | collective-permute-start | bytes 61448 | tf_op jit(solution)/shard_map/ppermute | solution.py:390
  9.3 2.6 %collective-permute-start.5 = (f32[40,128]{1,0:T(8,128)S(1)}, f32[40,128]{1,0:T(8,128)S(1)}, u32[]{:S(2)}, u32[]{:S(2)}) collective-permute-start(f32[40,128]{1,0:T(8,128)S(1)} %shard_map.66.refs_5_), channel_id=1, source_target_pairs={{0,8},{1,9},{2,10},{3,11},{4,0},{5,1},{6,2},{7,3},{8,16},{9,17},{1... | collective-permute-start | bytes 61448 | tf_op jit(solution)/shard_map/ppermute | solution.py:389
  12.1 3.1 %collective-permute-start.6 = (f32[40,128]{1,0:T(8,128)S(1)}, f32[40,128]{1,0:T(8,128)S(1)}, u32[]{:S(2)}, u32[]{:S(2)}) collective-permute-start(f32[40,128]{1,0:T(8,128)S(1)} %shard_map.68.iterate_ref), channel_id=1, source_target_pairs={{0,4},{1,5},{2,6},{3,7},{4,0},{5,1},{6,2},{7,3},{8,12},{9,13},{10,... | collective-permute-start | bytes 61448 | tf_op jit(solution)/shard_map/ppermute | solution.py:390
  13.3 3.5 %collective-permute-start.7 = (f32[40,128]{1,0:T(8,128)S(1)}, f32[40,128]{1,0:T(8,128)S(1)}, u32[]{:S(2)}, u32[]{:S(2)}) collective-permute-start(f32[40,128]{1,0:T(8,128)S(1)} %shard_map.68.iterate_ref), channel_id=1, source_target_pairs={{0,1},{1,0},{2,3},{3,2},{4,8},{5,9},{6,10},{7,11},{8,4},{9,5},{10,... | collective-permute-start | bytes 61448 | tf_op jit(solution)/shard_map/ppermute | solution.py:389
  17.0 2.1 %collective-permute-start.8 = (f32[40,128]{1,0:T(8,128)S(1)}, f32[40,128]{1,0:T(8,128)S(1)}, u32[]{:S(2)}, u32[]{:S(2)}) collective-permute-start(f32[40,128]{1,0:T(8,128)S(1)} %shard_map.70.iterate_ref), channel_id=1, source_target_pairs={{0,4},{1,5},{2,6},{3,7},{4,0},{5,1},{6,2},{7,3},{8,12},{9,13},{10,... | collective-permute-start | bytes 61448 | tf_op jit(solution)/shard_map/ppermute | solution.py:390
  17.4 3.5 %collective-permute-start.9 = (f32[40,128]{1,0:T(8,128)S(1)}, f32[40,128]{1,0:T(8,128)S(1)}, u32[]{:S(2)}, u32[]{:S(2)}) collective-permute-start(f32[40,128]{1,0:T(8,128)S(1)} %shard_map.70.iterate_ref), channel_id=1, source_target_pairs={{0,1},{1,0},{2,3},{3,2},{4,8},{5,9},{6,10},{7,11},{8,4},{9,5},{10,... | collective-permute-start | bytes 61448 | tf_op jit(solution)/shard_map/ppermute | solution.py:389
  21.1 1.5 %collective-permute-start.10 = (f32[40,128]{1,0:T(8,128)S(1)}, f32[40,128]{1,0:T(8,128)S(1)}, u32[]{:S(2)}, u32[]{:S(2)}) collective-permute-start(f32[40,128]{1,0:T(8,128)S(1)} %shard_map.72.iterate_ref), channel_id=1, source_target_pairs={{0,4},{1,5},{2,6},{3,7},{4,0},{5,1},{6,2},{7,3},{8,12},{9,13},{10,... | collective-permute-start | bytes 61448 | tf_op jit(solution)/shard_map/ppermute | solution.py:390
  21.6 3.5 %collective-permute-start.11 = (f32[40,128]{1,0:T(8,128)S(1)}, f32[40,128]{1,0:T(8,128)S(1)}, u32[]{:S(2)}, u32[]{:S(2)}) collective-permute-start(f32[40,128]{1,0:T(8,128)S(1)} %shard_map.72.iterate_ref), channel_id=1, source_target_pairs={{0,1},{1,0},{2,3},{3,2},{4,8},{5,9},{6,10},{7,11},{8,4},{9,5},{10,... | collective-permute-start | bytes 61448 | tf_op jit(solution)/shard_map/ppermute | solution.py:389
  22.6 5.6 %copy-start = (f32[15,3]{0,1:T(4,128)S(1)}, f32[15,3]{0,1:T(4,128)}, u32[]{:S(2)}) copy-start(f32[15,3]{0,1:T(4,128)} %param.8) | copy-start | bytes 544
  25.2 3.2 %collective-permute-start.12 = (f32[40,128]{1,0:T(8,128)S(1)}, f32[40,128]{1,0:T(8,128)S(1)}, u32[]{:S(2)}, u32[]{:S(2)}) collective-permute-start(f32[40,128]{1,0:T(8,128)S(1)} %shard_map.74.iterate_ref), channel_id=1, source_target_pairs={{0,4},{1,5},{2,6},{3,7},{4,0},{5,1},{6,2},{7,3},{8,12},{9,13},{10,... | collective-permute-start | bytes 61448 | tf_op jit(solution)/shard_map/ppermute | solution.py:390
  25.7 5.1 %collective-permute-start.13 = (f32[40,128]{1,0:T(8,128)S(1)}, f32[40,128]{1,0:T(8,128)S(1)}, u32[]{:S(2)}, u32[]{:S(2)}) collective-permute-start(f32[40,128]{1,0:T(8,128)S(1)} %shard_map.74.iterate_ref), channel_id=1, source_target_pairs={{4,8},{5,9},{6,10},{7,11},{8,4},{9,5},{10,6},{11,7},{12,16},{13,17... | collective-permute-start | bytes 61448 | tf_op jit(solution)/shard_map/ppermute | solution.py:389
